TPU v7x, 32 devices: a whole 2x2x4 slice. The times are simulated.
32 devices in a mesh: dp: 4 (over z), fsdp: 8 (over y, x, core).
Axes of the slice: x: 2, y: 2, z: 4, core: 2. Of those that a mesh axis runs over, the one named last changes fastest.
Arguments:
- replica_grads: bfloat16 [4, 8192, 4096], P('dp', 'fsdp'), may hold values from -4 to 4
- slot_table: int32 [32], replicated, may hold values from 0 to 39, as said below
- left_gram_state: float32 [40, 1, 4, 256, 1024], P('fsdp', None, 'dp')
- right_gram_state: float32 [40, 1, 4, 256, 1024], P('fsdp', None, 'dp')
- left_inverse_root: bfloat16 [40, 1, 4, 256, 1024], P('fsdp', None, 'dp')
- right_inverse_root: bfloat16 [40, 1, 4, 256, 1024], P('fsdp', None, 'dp')
Outputs:
- direction: bfloat16 [8, 4, 256, 4096], P('fsdp', 'dp')
- left_new: float32 [40, 1, 4, 256, 1024], P('fsdp', None, 'dp')
- right_new: float32 [40, 1, 4, 256, 1024], P('fsdp', None, 'dp')
Inputs may be any that keep to these rules, and one draw needn't show every extreme that they name: `slot_table`: the entries are distinct; slot v belongs to owner v // 5 of the flat shards' devices; some owner holds 5 blocks.
All inputs are finite; a program needn't handle non-finite values.
Results may differ from a plain program's by a relative error of at most 0.02.
Values may be sent and summed in bfloat16 or wider, within the bound.
A program may use at most 192 MiB of HBM per device.

v0:
```python
import jax
import jax.numpy as jnp
from jax import lax
from jax.sharding import PartitionSpec as P


def on_device(
    replica_grads,
    slot_table,
    left_gram_state,
    right_gram_state,
    left_inverse_root,
    right_inverse_root,
):
    slots_here = left_gram_state.shape[0]
    sub_blocks = left_gram_state.shape[1]
    strip_rows = left_gram_state.shape[3]
    block_size = left_gram_state.shape[4]
    band_rows = replica_grads.shape[1]
    model_width = replica_grads.shape[2]
    per_band = model_width // block_size
    shards = lax.axis_size("fsdp")
    groups = lax.axis_size("dp")
    total_slots = shards * slots_here
    block_count = slot_table.shape[0]
    band_index = lax.axis_index("fsdp")
    strip_index = lax.axis_index("dp")
    slot_indices = jnp.arange(total_slots, dtype=jnp.int32)
    summed = lax.psum_scatter(
        replica_grads[0].astype(jnp.float32).astype(jnp.bfloat16),
        "dp",
        scatter_dimension=0,
        tiled=True,
    )
    row_block = band_index * band_rows // block_size
    targets = lax.dynamic_slice_in_dim(slot_table, row_block * per_band, per_band, 0)
    chooser = (targets[:, None] == slot_indices[None, :]).astype(jnp.bfloat16)
    own_slots = band_index * slots_here + jnp.arange(slots_here, dtype=jnp.int32)
    holder = slot_table[None, :] == own_slots[:, None]
    occupied = jnp.any(holder, axis=1)
    block_of = jnp.sum(
        jnp.where(holder, jnp.arange(block_count, dtype=jnp.int32)[None, :], 0), axis=1
    )
    first_band = block_of // per_band * sub_blocks
    col_block = block_of % per_band
    all_bands = lax.all_gather(summed[None], "fsdp", axis=0, tiled=True)
    owned_rows = jax.vmap(
        lambda offset, column: lax.dynamic_slice(
            all_bands, (offset, 0, column * block_size), (sub_blocks, strip_rows, block_size)
        )
    )(first_band, col_block)
    owned_rows = owned_rows * occupied[:, None, None, None].astype(jnp.bfloat16)
    owned_rows = owned_rows.reshape(slots_here, sub_blocks, 1, strip_rows, block_size)
    entire = lax.all_gather(owned_rows, "dp", axis=2, tiled=True).reshape(
        slots_here, block_size, block_size
    )
    my_rows = owned_rows.reshape(slots_here, sub_blocks * strip_rows, block_size)
    left_gram = jnp.einsum("mrc,mnc->mrn", my_rows, entire, preferred_element_type=jnp.float32)
    left_new = left_gram_state + (left_gram / block_size).reshape(left_gram_state.shape)
    my_columns = lax.dynamic_index_in_dim(
        entire.reshape(slots_here, block_size, sub_blocks, groups, strip_rows),
        strip_index,
        3,
        keepdims=False,
    )
    my_columns = my_columns.reshape(slots_here, block_size, sub_blocks * strip_rows)
    right_gram = jnp.einsum("mnr,mnc->mrc", my_columns, entire, preferred_element_type=jnp.float32)
    right_new = right_gram_state + (right_gram / block_size).reshape(right_gram_state.shape)
    left_rows = left_inverse_root.reshape(slots_here, sub_blocks * strip_rows, block_size)
    mixed_rows = jnp.einsum(
        "mrn,mnc->mrc", left_rows, entire, preferred_element_type=jnp.float32
    ).astype(jnp.bfloat16)
    mixed_split = mixed_rows.reshape(
        slots_here, sub_blocks * strip_rows, sub_blocks, groups, strip_rows
    )
    result = jnp.einsum(
        "mrqjt,mqjtc->mrc",
        mixed_split,
        lax.all_gather(right_inverse_root, "dp", axis=2, tiled=True),
        preferred_element_type=jnp.float32,
    )
    outcome = result.astype(jnp.bfloat16).reshape(slots_here, sub_blocks, strip_rows, block_size)
    homeward = jax.vmap(
        lambda portion, offset: lax.dynamic_update_slice_in_dim(
            jnp.zeros((shards, strip_rows, block_size), jnp.bfloat16), portion, offset, 0
        ),
        out_axes=1,
    )(outcome, first_band)
    returned = lax.all_to_all(homeward, "fsdp", split_axis=0, concat_axis=0, tiled=True)
    picked = jnp.einsum(
        "cn,ntb->tcb",
        chooser,
        returned.reshape(total_slots, strip_rows, block_size),
        preferred_element_type=jnp.float32,
    ).astype(jnp.bfloat16)
    direction = picked.reshape(1, 1, strip_rows, model_width)
    return (direction, left_new, right_new)


def solution(mesh):
    placed = (
        P("dp", "fsdp", None),
        P(),
        P("fsdp", None, "dp", None, None),
        P("fsdp", None, "dp", None, None),
        P("fsdp", None, "dp", None, None),
        P("fsdp", None, "dp", None, None),
    )
    return jax.shard_map(
        on_device,
        mesh=mesh,
        in_specs=placed,
        out_specs=(
            P("fsdp", "dp", None, None),
            P("fsdp", None, "dp", None, None),
            P("fsdp", None, "dp", None, None),
        ),
        check_vma=False,
    )
```

profile of v0, /device:TPU:0, one launch (start us, length us, event | category | flops | bytes accessed | tf_op | source)
XLA Modules:
  0.0 976.8 jit_solution(10129963581104067872)
XLA Ops:
  8.0 149.7 %reduce-scatter.2.cloned.1.call-done = bf16[256,4096]{1,0:T(8,128)(2,1)} async-done(((bf16[1024,4096]{1,0:T(8,128)(2,1)}), bf16[256,4096]{1,0:T(8,128)(2,1)}) %reduce-scatter.2.cloned.1.call-update) | async-done | bytes 2097168 | tf_op jit(solution)/shard_map/reduce_scatter | solution.py:29
  158.3 91.7 %all-gather.9.cloned.1.call-done = bf16[2048,4096]{1,0:T(8,128)(2,1)} async-done(((bf16[256,4096]{1,0:T(8,128)(2,1)}), bf16[2048,4096]{1,0:T(8,128)(2,1)}) %all-gather.9.cloned.1.call-update) | async-done | bytes 16777232 | tf_op jit(solution)/shard_map/all_gather | solution.py:46
  250.0 19.5 %while.2 = (s32[]{:T(128)}, bf16[8,256,4096]{2,1,0:T(8,128)(2,1)}, s32[5,3]{0,1:T(4,128)S(1)}, bf16[5,1,256,1024]{3,2,1,0:T(8,128)(2,1)}, s32[]{:T(128)}) while((s32[]{:T(128)}, bf16[8,256,4096]{2,1,0:T(8,128)(2,1)}, s32[5,3]{0,1:T(4,128)S(1)}, bf16[5,1,256,1024]{3,2,1,0:T(8,128)(2,1)}, s32[]{:T(128)}) %tuple.63), condition=%wide.while_cond, body=%wide.while_body.sunk | while | flops 2 | bytes 1049717 | solution.py:48
  273.5 183.4 %all-gather.5.cloned.1.call-done = bf16[5,1,4,256,1024]{4,3,1,0,2:T(8,128)(2,1)} async-done(((bf16[5,1,1,256,1024]{4,3,1,0,2:T(8,128)(2,1)}), bf16[5,1,4,256,1024]{4,3,1,0,2:T(8,128)(2,1)}) %all-gather.5.cloned.1.call-update) | async-done | bytes 10485776 | tf_op jit(solution)/shard_map/all_gather | solution.py:54
  457.0 17.4 %copy.48 = bf16[5,1,4,256,1024]{3,2,4,0,1:T(4,128)(2,1)} copy(bf16[5,1,4,256,1024]{4,3,1,0,2:T(8,128)(2,1)} %all-gather.5.cloned.1.call-done) | data formatting | bytes 20971520 | tf_op jit(solution)/shard_map/all_gather | solution.py:54
  474.3 17.6 %reshape.158 = bf16[5,1024,1024]{1,2,0:T(8,128)(2,1)} reshape(bf16[5,1,4,256,1024]{3,2,4,0,1:T(4,128)(2,1)} %copy.48) | data formatting | bytes 20971520 | tf_op jit(solution)/shard_map/reshape | solution.py:54
  491.9 8.5 fusion.16
  500.4 140.1 %all-gather.7.cloned.1.call-done = bf16[5,1,4,256,1024]{4,3,2,0,1:T(8,128)(2,1)} async-done(((bf16[5,1,1,256,1024]{4,3,2,0,1:T(8,128)(2,1)}), bf16[5,1,4,256,1024]{4,3,2,0,1:T(8,128)(2,1)}) %all-gather.7.cloned.1.call-update) | async-done | bytes 10485776 | tf_op jit(solution)/shard_map/all_gather | solution.py:79
  640.5 9.3 fusion.6
  649.8 7.4 broadcast_in_dim.18.clone
  657.1 52.1 %while.3 = (s32[]{:T(128)}, bf16[5,8,256,1024]{3,2,0,1:T(8,128)(2,1)}, s32[5,4]{0,1:T(4,128)S(1)}, bf16[5,1,256,1024]{3,2,1,0:T(8,128)(2,1)}, s32[]{:T(128)}, /*index=5*/s32[4]{0:T(128)S(1)}) while((s32[]{:T(128)}, bf16[5,8,256,1024]{3,2,0,1:T(8,128)(2,1)}, s32[5,4]{0,1:T(4,128)S(1)}, bf16[5,1,256,1024]{3,2,1,0:T(8,128)(2,1)}, s32[]{:T(128)}, ...), condition=%wide.while_cond.1, body=%wide.while_body.1.sunk | while | flops 262173 | bytes 2623166 | solution.py:84
  663.6 4.0 bitcast_dynamic-update-slice_fusion.5
  684.4 4.0 bitcast_dynamic-update-slice_fusion.5
  694.8 4.0 bitcast_dynamic-update-slice_fusion.5
  709.2 6.3 all-to-all-start
  715.6 9.7 copy.56
  725.3 17.9 %reshape_reshape.4 = bf16[5,1024,1,4,256]{4,3,1,0,2:T(4,128)(2,1)} reshape(bf16[5,1,4,256,1024]{4,3,2,0,1:T(8,128)(2,1)} %copy.56) | data formatting | bytes 20971520 | tf_op jit(solution)/shard_map/reshape;reshape | solution.py:61
  743.2 8.7 constant_dynamic-slice_fusion.3
  751.8 11.1 %copy.57 = bf16[5,1024,1,1,256]{1,4,0,3,2:T(8,128)(2,1)} copy(bf16[5,1024,1,1,256]{4,3,1,0,2:T(2,128)(2,1)} %constant_dynamic-slice_fusion.3) | data formatting | bytes 5242880 | tf_op jit(solution)/shard_map/jit(dynamic_index_in_dim)/dynamic_slice | solution.py:60
  763.0 11.7 %fusion.4 = f32[5,1,1,256,1024]{4,3,2,1,0:T(8,128)} fusion(f32[5,1,1,256,1024]{4,3,2,1,0:T(8,128)} %param.9, bf16[5,1024,1024]{1,2,0:T(8,128)(2,1)} %reshape.158, bf16[5,1024,1,1,256]{1,4,0,3,2:T(8,128)(2,1)} %copy.57), kind=kOutput, calls=%fused_computation.12 | convolution fusion | flops 2686976000 | bytes 23592960 | tf_op jit(solution)/shard_map/mnr,mnc->mrc/dot_general | solution.py:67
  774.6 9.6 fusion.5
  784.2 160.0 %all-to-all-done = bf16[8,5,256,1024]{3,2,1,0:T(8,128)(2,1)} async-done(((bf16[8,5,256,1024]{3,2,1,0:T(8,128)(2,1)}), bf16[8,5,256,1024]{3,2,1,0:T(8,128)(2,1)}, u32[]{:S(2)}, u32[]{:S(2)}) %all-to-all-start) | async-done | bytes 20971552 | tf_op jit(solution)/shard_map/all_to_all | solution.py:89
  944.2 21.6 %convert_bitcast_fusion = bf16[256,4,1024]{2,1,0:T(4,128)(2,1)} fusion(bf16[40,256,1024]{2,1,0:T(8,128)(2,1)} %bitcast.14, s32[4]{0:T(128)S(1)} %dynamic_slice.7), kind=kOutput, calls=%fused_computation.24 | convolution fusion | flops 84934816 | bytes 23068688 | tf_op jit(solution)/shard_map/cn,ntb->tcb/dot_general | solution.py:90
  965.8 4.5 reshape.164
  (69 shorter events, 65.0 us)
Async XLA Ops:
  7.2 484.7 %copy-start = (bf16[5,1,1,256,1024]{4,3,2,1,0:T(8,128)(2,1)S(1)}, bf16[5,1,1,256,1024]{4,3,2,1,0:T(8,128)(2,1)}, u32[]{:S(2)}) copy-start(bf16[5,1,1,256,1024]{4,3,2,1,0:T(8,128)(2,1)} %param.10) | copy-start | bytes 7864324
  7.2 150.5 %reduce-scatter.2.cloned.1.call-start = ((), (), s32[]{:S(2)}) async-start(), calls=%async_computation.2 | async-start | bytes 10485760 | tf_op jit(solution)/shard_map/reduce_scatter | solution.py:29
  7.2 150.6 %copy-start.5 = (s32[32]{0:T(128)S(1)}, s32[32]{0:T(128)}, u32[]{:S(2)}) copy-start(s32[32]{0:T(128)} %param.7) | copy-start | bytes 388
  7.2 151.0 %copy-start.4 = (s32[3]{0:T(128)S(1)}, s32[3]{0:T(128)}, u32[]{:S(2)}) copy-start(s32[3]{0:T(128)} %constant.68.clone.1) | copy-start | bytes 40
  7.9 242.1 %all-gather.9.cloned.1.call-start = ((), (), s32[]{:S(2)}) async-start(), calls=%async_computation.5 | async-start | bytes 18874368 | tf_op jit(solution)/shard_map/all_gather | solution.py:46
  157.7 299.2 %all-gather.5.cloned.1.call-start = ((), (), s32[]{:S(2)}) async-start(), calls=%async_computation.3 | async-start | bytes 13107200 | tf_op jit(solution)/shard_map/all_gather | solution.py:54
  272.9 367.6 %all-gather.7.cloned.1.call-start = ((), (), s32[]{:S(2)}) async-start(), calls=%async_computation.4 | async-start | bytes 13107200 | tf_op jit(solution)/shard_map/all_gather | solution.py:79
  649.8 7.4 copy-start.3
  709.2 235.0 %all-to-all-start = ((bf16[8,5,256,1024]{3,2,1,0:T(8,128)(2,1)}), bf16[8,5,256,1024]{3,2,1,0:T(8,128)(2,1)}, u32[]{:S(2)}, u32[]{:S(2)}) async-start(bf16[8,5,256,1024]{3,2,1,0:T(8,128)(2,1)} %bitcast.125), calls=%async_computation.1 | async-start | bytes 41943040 | tf_op jit(solution)/shard_map/all_to_all | solution.py:89
  763.0 11.7 %copy-start.2 = (bf16[5,1,256,1024]{3,2,1,0:T(8,128)(2,1)S(1)}, bf16[5,1,256,1024]{3,2,1,0:T(8,128)(2,1)}, u32[]{:S(2)}) copy-start(bf16[5,1,256,1024]{3,2,1,0:T(8,128)(2,1)} %get-tuple-element.10) | copy-start | bytes 7864324
  944.2 26.0 %copy-start.1 = (bf16[5,1,1,256,1024]{4,3,2,1,0:T(8,128)(2,1)S(1)}, bf16[5,1,1,256,1024]{4,3,2,1,0:T(8,128)(2,1)}, u32[]{:S(2)}) copy-start(bf16[5,1,1,256,1024]{4,3,2,1,0:T(8,128)(2,1)} %param.10) | copy-start | bytes 7864324
Sparse Core Ops, SparseCore 0:
  10.3 147.3 reduce-scatter.1
  159.6 90.3 all-gather.8
  273.1 183.8 all-gather.4
  458.4 182.0 all-gather.6
where the time goes:
time: 980 us; the launch traced here: 977 us
  waiting for transfers between devices  726 us (74%)
  local copies, waits for them, and re-layouts  129 us (13%)
  matrix products  60.5 us (6%)
  other arithmetic  40.4 us (4%)
  between operations  13.9 us (1%)
    all_gather x1, waiting for transfers between devices, on_device(): lax.all_gather(owned_rows, 'dp', axis=2, tiled=True)  183 us
    all_to_all x1, waiting for transfers between devices, on_device(): lax.all_to_all(homeward, 'fsdp', split_axis=0, concat_axis=0, tiled=True)  160 us
    reduce_scatter x1, waiting for transfers between devices, on_device(): lax.psum_scatter(replica_grads[0].astype(jnp.float32).astype(jnp.bfloat16...  150 us
    all_gather x1, waiting for transfers between devices, on_device(): lax.all_gather(right_inverse_root, 'dp', axis=2, tiled=True)  140 us
    all_gather x1, waiting for transfers between devices, on_device(): all_bands = lax.all_gather(summed[None], 'fsdp', axis=0, tiled=True)  91.7 us
    scatter x10, other arithmetic  36.5 us
    all_gather x2, local copies, waits for them, and re-layouts, on_device(): lax.all_gather(owned_rows, 'dp', axis=2, tiled=True)  27 us
    dot_general x1, matrix products, on_device(): jnp.einsum('cn,ntb->tcb', chooser, returned.reshape(total_slots, strip_ro...  21.6 us
  transfers between devices with their start and end apart: 5, of which 5 were waited for; matrix products, arithmetic and copies ran while one was open for 12% of the time, Pallas kernels for 0%

commit v1 on v0

--- a/solution.py
+++ b/solution.py
@@ -73,12 +73,27 @@
     mixed_split = mixed_rows.reshape(
         slots_here, sub_blocks * strip_rows, sub_blocks, groups, strip_rows
     )
-    result = jnp.einsum(
+    length, place = (lax.axis_size("dp"), lax.axis_index("dp"))
+    left = [(i, (i - 1) % length) for i in range(length)]
+    rows = right_inverse_root.shape[2]
+    held = right_inverse_root
+    subtotal = jnp.einsum(
         "mrqjt,mqjtc->mrc",
-        mixed_split,
-        lax.all_gather(right_inverse_root, "dp", axis=2, tiled=True),
+        lax.dynamic_slice_in_dim(mixed_split, place * rows, held.shape[2], axis=3),
+        held,
         preferred_element_type=jnp.float32,
     )
+    for turn in range(1, length):
+        held = lax.ppermute(held, "dp", left)
+        subtotal = subtotal + jnp.einsum(
+            "mrqjt,mqjtc->mrc",
+            lax.dynamic_slice_in_dim(
+                mixed_split, (place + turn) % length * rows, held.shape[2], axis=3
+            ),
+            held,
+            preferred_element_type=jnp.float32,
+        )
+    result = subtotal
     outcome = result.astype(jnp.bfloat16).reshape(slots_here, sub_blocks, strip_rows, block_size)
     homeward = jax.vmap(
         lambda portion, offset: lax.dynamic_update_slice_in_dim(

time: 980 us -> 950 us (0.969)
  waiting for transfers between devices: 726 us -> 694 us
    ppermute x0 -> x3, waiting for transfers between devices: none -> 290 us  [on_device(): held = lax.ppermute(held, 'dp', left)]
    all_gather x1, waiting for transfers between devices: 183 us -> 1.52 us  [on_device(): lax.all_gather(owned_rows, 'dp', axis=2, tiled=True)]
    all_gather x1 -> x0, waiting for transfers between devices: 140 us -> none  [on_device(): lax.all_gather(right_inverse_root, 'dp', axis=2, tiled=True)]
  transfers between devices with their start and end apart: 5 -> 7, of which waited for: 5 -> 7; matrix products, arithmetic and copies ran while one was open for 12% -> 12% of each run, Pallas kernels for 0% -> 0%
where the time goes in v1:
time: 950 us; the launch traced here: 947 us
  waiting for transfers between devices  694 us (73%)
  local copies, waits for them, and re-layouts  131 us (14%)
  matrix products  58.9 us (6%)
  other arithmetic  39.8 us (4%)
  between operations  13.9 us (1%)
  starting transfers between devices  9.77 us (1%)
    ppermute x3, waiting for transfers between devices, on_device(): held = lax.ppermute(held, 'dp', left)  290 us
    all_to_all x1, waiting for transfers between devices, on_device(): lax.all_to_all(homeward, 'fsdp', split_axis=0, concat_axis=0, tiled=True)  160 us
    reduce_scatter x1, waiting for transfers between devices, on_device(): lax.psum_scatter(replica_grads[0].astype(jnp.float32).astype(jnp.bfloat16...  150 us
    all_gather x1, waiting for transfers between devices, on_device(): all_bands = lax.all_gather(summed[None], 'fsdp', axis=0, tiled=True)  91.7 us
    scatter x10, other arithmetic  35.9 us
    all_gather x2, local copies, waits for them, and re-layouts, on_device(): lax.all_gather(owned_rows, 'dp', axis=2, tiled=True)  26.6 us
    dot_general x1, matrix products, on_device(): jnp.einsum('cn,ntb->tcb', chooser, returned.reshape(total_slots, strip_ro...  21.6 us
    gather x15, local copies, waits for them, and re-layouts  20.3 us
  transfers between devices with their start and end apart: 7, of which 7 were waited for; matrix products, arithmetic and copies ran while one was open for 12% of the time, Pallas kernels for 0%

profile of v1, /device:TPU:0, one launch (start us, length us, event | category | flops | bytes accessed | tf_op | source)
XLA Modules:
  0.0 946.5 jit_solution(5097748173521850206)
XLA Ops:
  8.0 149.7 %reduce-scatter.2.cloned.1.call-done = bf16[256,4096]{1,0:T(8,128)(2,1)} async-done(((bf16[1024,4096]{1,0:T(8,128)(2,1)}), bf16[256,4096]{1,0:T(8,128)(2,1)}) %reduce-scatter.2.cloned.1.call-update) | async-done | bytes 2097168 | tf_op jit(solution)/shard_map/reduce_scatter | solution.py:29
  158.3 91.7 %all-gather.6.cloned.1.call-done = bf16[2048,4096]{1,0:T(8,128)(2,1)} async-done(((bf16[256,4096]{1,0:T(8,128)(2,1)}), bf16[2048,4096]{1,0:T(8,128)(2,1)}) %all-gather.6.cloned.1.call-update) | async-done | bytes 16777232 | tf_op jit(solution)/shard_map/all_gather | solution.py:46
  250.0 20.3 %while.2 = (s32[]{:T(128)}, bf16[8,256,4096]{2,1,0:T(8,128)(2,1)}, s32[5,3]{0,1:T(4,128)S(1)}, bf16[5,1,256,1024]{3,2,1,0:T(8,128)(2,1)}, s32[]{:T(128)}) while((s32[]{:T(128)}, bf16[8,256,4096]{2,1,0:T(8,128)(2,1)}, s32[5,3]{0,1:T(4,128)S(1)}, bf16[5,1,256,1024]{3,2,1,0:T(8,128)(2,1)}, s32[]{:T(128)}) %tuple.61), condition=%wide.while_cond, body=%wide.while_body.sunk | while | flops 2 | bytes 1049717 | solution.py:48
  277.2 147.5 %collective-permute-done = bf16[5,1,1,256,1024]{4,3,0,2,1:T(8,128)(2,1)S(1)} collective-permute-done((bf16[5,1,1,256,1024]{4,3,0,2,1:T(8,128)(2,1)}, bf16[5,1,1,256,1024]{4,3,0,2,1:T(8,128)(2,1)S(1)}, u32[]{:S(2)}, u32[]{:S(2)}) %collective-permute-start) | collective-permute-done | bytes 2621472 | tf_op jit(solution)/shard_map/ppermute | solution.py:87
  426.2 131.7 %collective-permute-done.1 = bf16[5,1,1,256,1024]{4,3,0,2,1:T(8,128)(2,1)} collective-permute-done((bf16[5,1,1,256,1024]{4,3,0,2,1:T(8,128)(2,1)S(1)}, bf16[5,1,1,256,1024]{4,3,0,2,1:T(8,128)(2,1)}, u32[]{:S(2)}, u32[]{:S(2)}) %collective-permute-start.1) | collective-permute-done | bytes 2621472 | tf_op jit(solution)/shard_map/ppermute | solution.py:87
  559.4 17.0 %copy.57 = bf16[5,1,4,256,1024]{3,2,4,0,1:T(4,128)(2,1)} copy(bf16[5,1,4,256,1024]{4,3,1,0,2:T(8,128)(2,1)} %all-gather.4.cloned.1.call-done) | data formatting | bytes 20971520 | tf_op jit(solution)/shard_map/all_gather | solution.py:54
  576.4 17.5 %reshape.177 = bf16[5,1024,1024]{1,2,0:T(8,128)(2,1)} reshape(bf16[5,1,4,256,1024]{3,2,4,0,1:T(4,128)(2,1)} %copy.57) | data formatting | bytes 20971520 | tf_op jit(solution)/shard_map/reshape | solution.py:54
  593.9 7.0 fusion.22
  605.6 10.7 %collective-permute-done.2 = bf16[5,1,1,256,1024]{4,3,0,2,1:T(8,128)(2,1)} collective-permute-done((bf16[5,1,1,256,1024]{4,3,0,2,1:T(8,128)(2,1)}, bf16[5,1,1,256,1024]{4,3,0,2,1:T(8,128)(2,1)}, u32[]{:S(2)}, u32[]{:S(2)}) %collective-permute-start.2) | collective-permute-done | bytes 2621472 | tf_op jit(solution)/shard_map/ppermute | solution.py:87
  616.4 4.5 fusion.4
  620.9 7.4 broadcast_in_dim.18.clone
  628.2 50.8 %while.3 = (s32[]{:T(128)}, bf16[5,8,256,1024]{3,2,0,1:T(8,128)(2,1)}, s32[5,4]{0,1:T(4,128)S(1)}, bf16[5,1,256,1024]{3,2,1,0:T(8,128)(2,1)}, s32[]{:T(128)}, /*index=5*/s32[4]{0:T(128)S(1)}) while((s32[]{:T(128)}, bf16[5,8,256,1024]{3,2,0,1:T(8,128)(2,1)}, s32[5,4]{0,1:T(4,128)S(1)}, bf16[5,1,256,1024]{3,2,1,0:T(8,128)(2,1)}, s32[]{:T(128)}, ...), condition=%wide.while_cond.1, body=%wide.while_body.1.sunk | while | flops 262173 | bytes 2623166 | solution.py:99
  654.7 4.0 bitcast_dynamic-update-slice_fusion.5
  664.9 4.0 bitcast_dynamic-update-slice_fusion.5
  679.0 6.3 all-to-all-start
  685.4 9.7 %copy.68 = bf16[5,1,4,256,1024]{4,3,2,0,1:T(8,128)(2,1)} copy(bf16[5,1,4,256,1024]{4,3,1,0,2:T(8,128)(2,1)} %all-gather.4.cloned.1.call-done) | data formatting | bytes 20971520 | tf_op jit(solution)/shard_map/all_gather | solution.py:54
  695.1 17.9 %reshape_reshape.4 = bf16[5,1024,1,4,256]{4,3,1,0,2:T(4,128)(2,1)} reshape(bf16[5,1,4,256,1024]{4,3,2,0,1:T(8,128)(2,1)} %copy.68) | data formatting | bytes 20971520 | tf_op jit(solution)/shard_map/reshape;reshape | solution.py:61
  712.9 8.7 constant_dynamic-slice_fusion.3
  721.6 11.1 %copy.69 = bf16[5,1024,1,1,256]{1,4,0,3,2:T(8,128)(2,1)} copy(bf16[5,1024,1,1,256]{4,3,1,0,2:T(2,128)(2,1)} %constant_dynamic-slice_fusion.3) | data formatting | bytes 5242880 | tf_op jit(solution)/shard_map/jit(dynamic_index_in_dim)/dynamic_slice | solution.py:60
  732.8 11.7 %fusion.2 = f32[5,1,1,256,1024]{4,3,2,1,0:T(8,128)} fusion(f32[5,1,1,256,1024]{4,3,2,1,0:T(8,128)} %param.9, bf16[5,1024,1024]{1,2,0:T(8,128)(2,1)} %reshape.177, bf16[5,1024,1,1,256]{1,4,0,3,2:T(8,128)(2,1)} %copy.69), kind=kOutput, calls=%fused_computation.10 | convolution fusion | flops 2686976000 | bytes 23592960 | tf_op jit(solution)/shard_map/mnr,mnc->mrc/dot_general | solution.py:67
  744.4 9.6 %fusion.3 = f32[5,1,1,256,1024]{4,3,2,1,0:T(8,128)} fusion(f32[5,1,1,256,1024]{4,3,2,1,0:T(8,128)} %param.8, bf16[5,1024,1024]{1,2,0:T(8,128)(2,1)} %reshape.177, bf16[5,1,256,1024]{3,2,1,0:T(8,128)(2,1)S(1)} %copy-done.2, bf16[5]{0:T(256)(128)(2,1)S(1)} %convert_element_type.26), kind=kOutput, calls=%fused_computation.12 | convolution fusion | flops 2688286720 | bytes 23592970 | tf_op jit(solution)/shard_map/mrc,mnc->mrn/dot_general | solution.py:58
  754.0 160.0 %all-to-all-done = bf16[8,5,256,1024]{3,2,1,0:T(8,128)(2,1)} async-done(((bf16[8,5,256,1024]{3,2,1,0:T(8,128)(2,1)}), bf16[8,5,256,1024]{3,2,1,0:T(8,128)(2,1)}, u32[]{:S(2)}, u32[]{:S(2)}) %all-to-all-start) | async-done | bytes 20971552 | tf_op jit(solution)/shard_map/all_to_all | solution.py:104
  914.0 21.6 %convert_bitcast_fusion = bf16[256,4,1024]{2,1,0:T(4,128)(2,1)} fusion(bf16[40,256,1024]{2,1,0:T(8,128)(2,1)} %bitcast.20, s32[4]{0:T(128)S(1)} %dynamic_slice.23), kind=kOutput, calls=%fused_computation.30 | convolution fusion | flops 84934816 | bytes 23068688 | tf_op jit(solution)/shard_map/cn,ntb->tcb/dot_general | solution.py:105
  935.6 4.5 reshape.190
  (81 shorter events, 79.0 us)
Async XLA Ops:
  7.2 586.8 %copy-start = (bf16[5,1,1,256,1024]{4,3,2,1,0:T(8,128)(2,1)S(1)}, bf16[5,1,1,256,1024]{4,3,2,1,0:T(8,128)(2,1)}, u32[]{:S(2)}) copy-start(bf16[5,1,1,256,1024]{4,3,2,1,0:T(8,128)(2,1)} %param.10) | copy-start | bytes 7864324
  7.2 150.5 %reduce-scatter.2.cloned.1.call-start = ((), (), s32[]{:S(2)}) async-start(), calls=%async_computation.2 | async-start | bytes 10485760 | tf_op jit(solution)/shard_map/reduce_scatter | solution.py:29
  7.2 150.6 %copy-start.8 = (s32[32]{0:T(128)S(1)}, s32[32]{0:T(128)}, u32[]{:S(2)}) copy-start(s32[32]{0:T(128)} %param.7) | copy-start | bytes 388
  7.2 151.0 %copy-start.7 = (s32[3]{0:T(128)S(1)}, s32[3]{0:T(128)}, u32[]{:S(2)}) copy-start(s32[3]{0:T(128)} %constant.85.clone.1) | copy-start | bytes 40
  7.9 242.1 %all-gather.6.cloned.1.call-start = ((), (), s32[]{:S(2)}) async-start(), calls=%async_computation.4 | async-start | bytes 18874368 | tf_op jit(solution)/shard_map/all_gather | solution.py:46
  157.7 401.7 %all-gather.4.cloned.1.call-start = ((), (), s32[]{:S(2)}) async-start(), calls=%async_computation.3 | async-start | bytes 13107200 | tf_op jit(solution)/shard_map/all_gather | solution.py:54
  273.8 150.9 %collective-permute-start = (bf16[5,1,1,256,1024]{4,3,0,2,1:T(8,128)(2,1)}, bf16[5,1,1,256,1024]{4,3,0,2,1:T(8,128)(2,1)S(1)}, u32[]{:S(2)}, u32[]{:S(2)}) collective-permute-start(bf16[5,1,1,256,1024]{4,3,0,2,1:T(8,128)(2,1)} %bitcast.150), channel_id=1, source_target_pairs={{0,24},{8,0},{16,8},{24,16},{1,25},{9,1},{17,9},{25,17},{2,26},{10... | collective-permute-start | bytes 7864328 | tf_op jit(solution)/shard_map/ppermute | solution.py:87
  424.7 1.5 copy-start.4
  426.2 131.7 %collective-permute-start.1 = (bf16[5,1,1,256,1024]{4,3,0,2,1:T(8,128)(2,1)S(1)}, bf16[5,1,1,256,1024]{4,3,0,2,1:T(8,128)(2,1)}, u32[]{:S(2)}, u32[]{:S(2)}) collective-permute-start(bf16[5,1,1,256,1024]{4,3,0,2,1:T(8,128)(2,1)S(1)} %collective-permute-done), channel_id=1, source_target_pairs={{0,24},{8,0},{16,8},{24,16},{1,25},{9,1},{17,9},{25,17},{2,26},{10... | collective-permute-start | bytes 7864328 | tf_op jit(solution)/shard_map/ppermute | solution.py:87
  557.9 58.5 %collective-permute-start.2 = (bf16[5,1,1,256,1024]{4,3,0,2,1:T(8,128)(2,1)}, bf16[5,1,1,256,1024]{4,3,0,2,1:T(8,128)(2,1)}, u32[]{:S(2)}, u32[]{:S(2)}) collective-permute-start(bf16[5,1,1,256,1024]{4,3,0,2,1:T(8,128)(2,1)} %collective-permute-done.1), channel_id=1, source_target_pairs={{0,24},{8,0},{16,8},{24,16},{1,25},{9,1},{17,9},{25,17},{2,26},{10... | collective-permute-start | bytes 7864328 | tf_op jit(solution)/shard_map/ppermute | solution.py:87
  593.9 7.0 copy-start.3
  601.9 2.8 copy-start.5
  620.9 7.4 copy-start.6
  679.0 235.0 %all-to-all-start = ((bf16[8,5,256,1024]{3,2,1,0:T(8,128)(2,1)}), bf16[8,5,256,1024]{3,2,1,0:T(8,128)(2,1)}, u32[]{:S(2)}, u32[]{:S(2)}) async-start(bf16[8,5,256,1024]{3,2,1,0:T(8,128)(2,1)} %bitcast.144), calls=%async_computation.1 | async-start | bytes 41943040 | tf_op jit(solution)/shard_map/all_to_all | solution.py:104
  732.7 11.7 %copy-start.2 = (bf16[5,1,256,1024]{3,2,1,0:T(8,128)(2,1)S(1)}, bf16[5,1,256,1024]{3,2,1,0:T(8,128)(2,1)}, u32[]{:S(2)}) copy-start(bf16[5,1,256,1024]{3,2,1,0:T(8,128)(2,1)} %get-tuple-element.10) | copy-start | bytes 7864324
  914.0 26.0 %copy-start.1 = (bf16[5,1,1,256,1024]{4,3,2,1,0:T(8,128)(2,1)S(1)}, bf16[5,1,1,256,1024]{4,3,2,1,0:T(8,128)(2,1)}, u32[]{:S(2)}) copy-start(bf16[5,1,1,256,1024]{4,3,2,1,0:T(8,128)(2,1)} %param.10) | copy-start | bytes 7864324
Sparse Core Ops, SparseCore 0:
  10.3 147.3 reduce-scatter.1
  159.6 90.3 all-gather.5
  273.9 285.4 all-gather.3
